TPU v7x, 32 devices: a whole 2x2x4 slice. The times are simulated.
32 devices in a mesh: rows: 4 (over z), model: 8 (over y, x, core).
Axes of the slice: x: 2, y: 2, z: 4, core: 2. Of those that a mesh axis runs over, the one named last changes fastest.
Arguments:
- train_query: bfloat16 [8192, 8192], P('rows', 'model'), may hold values from -0.0625 to 0.0625
- low_query: bfloat16 [8192, 16], P('rows'), may hold values from -0.0625 to 0.0625
- high_query: bfloat16 [16, 8192], P(None, 'model'), may hold values from -1.5 to 1.5
- train_key: bfloat16 [8192, 1024], P('rows', 'model'), may hold values from -0.0625 to 0.0625
- low_key: bfloat16 [8192, 16], P('rows'), may hold values from -0.0625 to 0.0625
- high_key: bfloat16 [16, 1024], P(None, 'model'), may hold values from -1.5 to 1.5
- train_value: bfloat16 [8192, 1024], P('rows', 'model'), may hold values from -0.0625 to 0.0625
- low_value: bfloat16 [8192, 16], P('rows'), may hold values from -0.0625 to 0.0625
- high_value: bfloat16 [16, 1024], P(None, 'model'), may hold values from -1.5 to 1.5
- train_mixed: bfloat16 [8192, 8192], P('model', 'rows'), may hold values from -0.0625 to 0.0625
- low_mixed: bfloat16 [8192, 16], P('model'), may hold values from -0.0625 to 0.0625
- high_mixed: bfloat16 [16, 8192], P(None, 'rows'), may hold values from -1.5 to 1.5
- norm_train: float32 [8192], P(('rows', 'model')), may hold values from 0.25 to 1.75
- norm_step: float32 [8192], P(('rows', 'model')), may hold values from -0.3 to 0.3
Outputs:
- serving_query: bfloat16 [8192, 8192], P('model')
- serving_key: bfloat16 [1024, 8192], P('model')
- serving_value: bfloat16 [1024, 8192], P('model')
- serving_mixed: bfloat16 [8192, 8192], P(None, 'model')
- serve_norm: bfloat16 [8192], replicated
All inputs are finite; a program needn't handle non-finite values.
Results may differ from a plain program's by a relative error of at most 0.001.
Values may be sent and summed in bfloat16 or wider, within the bound.
A program may use at most 128 MiB of HBM per device.

v0:
```python
import jax
import jax.numpy as jnp
from jax import lax
from jax.sharding import PartitionSpec as P

mix_rate = 0.5


def body(
    train_query,
    low_query,
    high_query,
    train_key,
    low_key,
    high_key,
    train_value,
    low_value,
    high_value,
    train_mixed,
    low_mixed,
    high_mixed,
    norm_train,
    norm_step,
):
    whole_query = train_query.astype(jnp.float32) + mix_rate * jnp.dot(
        low_query, high_query, preferred_element_type=jnp.float32
    )
    whole_key = train_key.astype(jnp.float32) + mix_rate * jnp.dot(
        low_key, high_key, preferred_element_type=jnp.float32
    )
    whole_value = train_value.astype(jnp.float32) + mix_rate * jnp.dot(
        low_value, high_value, preferred_element_type=jnp.float32
    )
    whole_mixed = train_mixed.astype(jnp.float32) + mix_rate * jnp.dot(
        low_mixed, high_mixed, preferred_element_type=jnp.float32
    )
    narrow_query, narrow_key, narrow_value, narrow_mixed = (
        whole_query.astype(jnp.bfloat16),
        whole_key.astype(jnp.bfloat16),
        whole_value.astype(jnp.bfloat16),
        whole_mixed.astype(jnp.bfloat16),
    )
    serving_query, serving_key, serving_value, serving_mixed = (
        lax.all_gather(narrow_query, "rows", axis=0, tiled=True),
        lax.all_gather(narrow_key, "rows", axis=0, tiled=True),
        lax.all_gather(narrow_value, "rows", axis=0, tiled=True),
        lax.all_gather(narrow_mixed, "rows", axis=1, tiled=True),
    )
    serving_query, serving_key, serving_value, serving_mixed = (
        serving_query.T,
        serving_key.T,
        serving_value.T,
        serving_mixed.T,
    )
    serve_norm = lax.all_gather(
        (norm_train + norm_step).astype(jnp.bfloat16), ("rows", "model"), axis=0, tiled=True
    )
    return (serving_query, serving_key, serving_value, serving_mixed, serve_norm)


def solution(mesh):
    return jax.shard_map(
        body,
        mesh=mesh,
        in_specs=(
            P("rows", "model"),
            P("rows", None),
            P(None, "model"),
            P("rows", "model"),
            P("rows", None),
            P(None, "model"),
            P("rows", "model"),
            P("rows", None),
            P(None, "model"),
            P("model", "rows"),
            P("model", None),
            P(None, "rows"),
            P(("rows", "model")),
            P(("rows", "model")),
        ),
        out_specs=(P("model", None), P("model", None), P("model", None), P(None, "model"), P()),
        check_vma=False,
    )
```

profile of v0, /device:TPU:0, one launch (start us, length us, event | category | flops | bytes accessed | tf_op | source)
XLA Modules:
  0.0 708.4 jit_solution(878410896328785297)
XLA Ops:
  7.2 0.0 copy-start
  7.2 0.0 copy-start.3
  7.2 0.0 all-gather.8.cloned.1.call-start
  7.3 2.2 fusion.2
  9.5 0.0 all-gather.8.cloned.1.call-update
  9.5 0.0 all-gather.10.cloned.1.call-start
  9.6 2.2 fusion.3
  11.8 0.0 all-gather.10.cloned.1.call-update
  11.8 0.0 all-gather.6.cloned.1.call-start
  11.9 5.5 add_convert_fusion.1
  17.4 0.0 all-gather.6.cloned.1.call-update
  17.4 0.0 all-gather.12.cloned.1.call-start
  17.5 5.6 add_convert_fusion
  23.1 0.0 all-gather.12.cloned.1.call-update
  23.2 45.0 %all-gather = bf16[32,1,256]{2,1,0:T(2,128)(2,1)S(1)} all-gather(bf16[1,1,256]{2,1,0:T(2,128)(2,1)S(1)} %reshape.10), channel_id=1, replica_groups=mesh['rows'=4,'model'=8] {'rows','model'}, dimensions={0}, use_global_device_ids=true | all-gather | bytes 16896 | tf_op jit(solution)/shard_map/all_gather | solution.py:55
  68.2 0.1 reduce
  68.3 0.6 copy.31
  68.9 4.1 copy.28
  73.0 32.4 %all-gather.10.cloned.1.call-done = bf16[8192,128]{1,0:T(8,128)(2,1)} async-done(((bf16[2048,128]{1,0:T(8,128)(2,1)}), bf16[8192,128]{1,0:T(8,128)(2,1)}) %all-gather.10.cloned.1.call-update) | async-done | bytes 2097168 | tf_op jit(solution)/shard_map/all_gather | solution.py:46
  105.4 4.1 copy.29
  109.4 283.7 %all-gather.6.cloned.1.call-done = bf16[8192,1024]{1,0:T(8,128)(2,1)} async-done(((bf16[2048,1024]{1,0:T(8,128)(2,1)}), bf16[8192,1024]{1,0:T(8,128)(2,1)}) %all-gather.6.cloned.1.call-update) | async-done | bytes 16777232 | tf_op jit(solution)/shard_map/all_gather | solution.py:44
  393.1 21.9 %copy.27 = bf16[1024,8192]{1,0:T(8,128)(2,1)} copy(bf16[1024,8192]{0,1:T(8,128)(2,1)} %bitcast.14) | data formatting | bytes 33554432
  415.0 264.5 %all-gather.12.cloned.1.call-done = bf16[1024,8192]{1,0:T(8,128)(2,1)} async-done(((bf16[1024,2048]{1,0:T(8,128)(2,1)}), bf16[1024,8192]{1,0:T(8,128)(2,1)}) %all-gather.12.cloned.1.call-update) | async-done | bytes 16777232 | tf_op jit(solution)/shard_map/all_gather | solution.py:47
  679.5 22.4 %copy.30 = bf16[8192,1024]{1,0:T(8,128)(2,1)} copy(bf16[8192,1024]{0,1:T(8,128)(2,1)} %bitcast.15) | data formatting | bytes 33554432
  (13 shorter events, 0.0 us)
Async XLA Ops:
  7.2 4.7 copy-start
  7.2 10.3 %copy-start.3 = (bf16[1024,16]{0,1:T(8,128)(2,1)S(1)}, bf16[1024,16]{0,1:T(8,128)(2,1)}, u32[]{:S(2)}) copy-start(bf16[1024,16]{0,1:T(8,128)(2,1)} %param.24) | copy-start | bytes 98308
  7.2 10.3 %copy-start.2 = (bf16[16,2048]{1,0:T(8,128)(2,1)S(1)}, bf16[16,2048]{1,0:T(8,128)(2,1)}, u32[]{:S(2)}) copy-start(bf16[16,2048]{1,0:T(8,128)(2,1)} %param.25) | copy-start | bytes 196612
  7.2 61.7 %all-gather.8.cloned.1.call-start = ((), (), s32[]{:S(2)}) async-start(), calls=%async_computation.1 | async-start | bytes 2621440 | tf_op jit(solution)/shard_map/all_gather | solution.py:45
  9.5 95.9 %all-gather.10.cloned.1.call-start = ((), (), s32[]{:S(2)}) async-start(), calls=%async_computation.2 | async-start | bytes 2621440 | tf_op jit(solution)/shard_map/all_gather | solution.py:46
  11.8 381.3 %all-gather.6.cloned.1.call-start = ((), (), s32[]{:S(2)}) async-start(), calls=%async_computation | async-start | bytes 20971520 | tf_op jit(solution)/shard_map/all_gather | solution.py:44
  17.4 5.7 copy-start.4
  17.4 5.7 copy-start.5
  17.4 662.1 %all-gather.12.cloned.1.call-start = ((), (), s32[]{:S(2)}) async-start(), calls=%async_computation.3 | async-start | bytes 20971520 | tf_op jit(solution)/shard_map/all_gather | solution.py:47
  679.5 22.4 %copy-start.1 = (bf16[2048,16]{0,1:T(8,128)(2,1)S(1)}, bf16[2048,16]{0,1:T(8,128)(2,1)}, u32[]{:S(2)}) copy-start(bf16[2048,16]{0,1:T(8,128)(2,1)} %param.15) | copy-start | bytes 196612
Sparse Core Ops, SparseCore 0:
  10.2 48.5 all-gather.7
  60.9 44.4 all-gather.9
  107.5 285.5 all-gather.5
  394.5 284.9 all-gather.11
where the time goes:
time: 710 us; the launch traced here: 708 us
  waiting for transfers between devices  581 us (82%)
  local copies, waits for them, and re-layouts  53.1 us (7%)
  blocking collectives  45 us (6%)
  matrix products  15.6 us (2%)
  between operations  13.8 us (2%)
    all_gather x1, waiting for transfers between devices, body(): lax.all_gather(narrow_query, 'rows', axis=0, tiled=True)  284 us
    all_gather x1, waiting for transfers between devices, body(): lax.all_gather(narrow_mixed, 'rows', axis=1, tiled=True)  265 us
    unnamed x18, local copies, waits for them, and re-layouts  53.1 us
    all_gather x1, blocking collectives, body(): lax.all_gather((norm_train + norm_step).astype(jnp.bfloat16), ('rows', 'm...  45 us
    all_gather x1, waiting for transfers between devices, body(): lax.all_gather(narrow_value, 'rows', axis=0, tiled=True)  32.4 us
  transfers between devices with their start and end apart: 4, of which 3 were waited for; matrix products, arithmetic and copies ran while one was open for 6% of the time, Pallas kernels for 0%

commit v1 on v0

v1 whole, which is shorter than its diff:
```python
import jax
import jax.numpy as jnp
from jax import lax
from jax.experimental import pallas as pl
from jax.experimental.pallas import tpu as pltpu
from jax.sharding import PartitionSpec as P


mix_rate = 0.5


def merge_kernel(train_ref, low_ref, high_ref, out_ref):
    change = lax.dot_general(
        high_ref[...], low_ref[...], (((0,), (0,)), ((), ())), preferred_element_type=jnp.float32
    )
    whole = train_ref[...].T.astype(jnp.float32) + mix_rate * change
    out_ref[...] = whole.astype(out_ref.dtype)


def merged(train, low, high, part, parts):
    depth, width = train.shape
    rank = low.shape[1]
    tile = min(256 if depth <= 1024 else 128, width // parts)
    tiles = width // parts // tile
    return pl.pallas_call(
        merge_kernel,
        grid=(tiles,),
        in_specs=[
            pl.BlockSpec((depth, tile), lambda i: (0, part * tiles + i)),
            pl.BlockSpec((rank, depth), lambda i: (0, 0)),
            pl.BlockSpec((rank, tile), lambda i: (0, part * tiles + i)),
        ],
        out_specs=pl.BlockSpec((tile, depth), lambda i: (i, 0)),
        out_shape=jax.ShapeDtypeStruct((width // parts, depth), train.dtype),
        cost_estimate=pl.CostEstimate(
            flops=2 * rank * depth * width // parts,
            bytes_accessed=4 * depth * width // parts,
            transcendentals=0,
        ),
        name="merge",
    )(train, low.T, high)


def place_kernel(owner_ref, *refs):
    refs[-1][...] = refs[-2][...]


def placed(whole, piece, owner, shape, axis, part, parts):
    rows, width = piece.shape
    tile = min(rows, 256)
    tiles = rows // tile
    if axis == 1:
        spot = lambda i, owner: (part * tiles + i, owner[0])
    else:
        spot = lambda i, owner: ((owner[0] * parts + part) * tiles + i, 0)
    before = [] if whole is None else [whole]
    return pl.pallas_call(
        place_kernel,
        grid_spec=pltpu.PrefetchScalarGridSpec(
            num_scalar_prefetch=1,
            grid=(tiles,),
            in_specs=[pl.BlockSpec(memory_space=pl.ANY)] * len(before)
            + [pl.BlockSpec((tile, width), lambda i, owner: (i, 0))],
            out_specs=pl.BlockSpec((tile, width), spot),
        ),
        out_shape=jax.ShapeDtypeStruct(shape, piece.dtype),
        input_output_aliases={1: 0} if before else {},
        cost_estimate=pl.CostEstimate(
            flops=0, bytes_accessed=4 * rows * width, transcendentals=0
        ),
        name="place",
    )(owner, *before, piece)


def after(value, earlier):
    return lax.optimization_barrier((value, earlier))


def order(step, count):
    return list(range(count)) if step == 1 else list(range(2, count)) + [0, 1]


def body(
    train_query,
    low_query,
    high_query,
    train_key,
    low_key,
    high_key,
    train_value,
    low_value,
    high_value,
    train_mixed,
    low_mixed,
    high_mixed,
    norm_train,
    norm_step,
):
    n = lax.axis_size("rows")
    me = lax.axis_index("rows")
    ring = [(i, (i + 1) % n) for i in range(n)]
    owners = [jnp.reshape(lax.rem(me - step + n, n), (1,)).astype(jnp.int32) for step in range(n)]

    weights = {
        "key": (train_key, low_key, high_key, 1),
        "value": (train_value, low_value, high_value, 1),
        "query": (train_query, low_query, high_query, 1),
        "mixed": (train_mixed, low_mixed, high_mixed, 0),
    }
    plan = [
        ("key", 0, 1),
        ("value", 0, 1),
        ("query", 0, 2),
        ("query", 1, 2),
        ("mixed", 0, 2),
        ("mixed", 1, 2),
    ]
    shapes, outs = {}, {}
    for name, (train, _, _, axis) in weights.items():
        shape = [train.shape[1], train.shape[0]]
        shape[axis] *= n
        shapes[name] = tuple(shape)
        outs[name] = None

    def place(number, piece, step):
        name, part, parts = plan[number]
        outs[name] = placed(
            outs[name], piece, owners[step], shapes[name], weights[name][3], part, parts
        )
        return name

    gain = (norm_train + norm_step).astype(jnp.bfloat16)
    gain = lax.all_gather(gain, "model", axis=0, tiled=True)

    own = []
    for name, part, parts in plan:
        train, low, high, _ = weights[name]
        if own:
            high, own[-1] = after(high, own[-1])
        own.append(merged(train, low, high, part, parts))
    moving = list(own)
    serve_norm = lax.dynamic_update_slice_in_dim(
        jnp.zeros((n, gain.shape[0]), gain.dtype), gain[None], me, 0
    )
    last = None
    for step in range(1, n):
        turn = order(step, len(plan))
        arrived = {}
        for number in turn:
            piece = moving[number]
            if last is not None:
                piece, outs[last] = after(piece, outs[last])
            arrived[number] = lax.ppermute(piece, "rows", ring)
            if step > 1:
                last = place(number, piece, step - 1)
        if step == 1:
            for number in turn:
                last = place(number, own[number], 0)
        gain = lax.ppermute(gain, "rows", ring)
        serve_norm = lax.dynamic_update_slice_in_dim(
            serve_norm, gain[None], owners[step][0], 0
        )
        moving = [arrived[number] for number in range(len(plan))]
    for number in order(n - 1, len(plan)):
        place(number, moving[number], n - 1)
    serve_norm = jnp.reshape(serve_norm, (-1,))
    return (outs["query"], outs["key"], outs["value"], outs["mixed"], serve_norm)


def solution(mesh):
    return jax.shard_map(
        body,
        mesh=mesh,
        in_specs=(
            P("rows", "model"),
            P("rows", None),
            P(None, "model"),
            P("rows", "model"),
            P("rows", None),
            P(None, "model"),
            P("rows", "model"),
            P("rows", None),
            P(None, "model"),
            P("model", "rows"),
            P("model", None),
            P(None, "rows"),
            P(("rows", "model")),
            P(("rows", "model")),
        ),
        out_specs=(P("model", None), P("model", None), P("model", None), P(None, "model"), P()),
        check_vma=False,
    )
```

time: 710 us -> 658 us (0.927)
  Pallas kernels: 0 us -> 88.8 us
  local copies, waits for them, and re-layouts: 53.1 us -> 2.61 us
  waiting for transfers between devices: 581 us -> 541 us
  blocking collectives: 45 us -> 9.16 us
  matrix products: 15.6 us -> 0 us
  starting transfers between devices: 0.16 us -> 14.8 us
  between operations: 13.8 us -> 0.78 us
    all_gather x4 -> x0, waiting for transfers between devices: 581 us -> none  [the longest x1 284 us: body(): lax.all_gather(narrow_query, 'rows', axis=0, tiled=True)]
    ppermute x0 -> x21, waiting for transfers between devices: none -> 541 us  [the longest x18 372 us: body(): arrived[number] = lax.ppermute(piece, 'rows', ring)]
    pallas_call x0 -> x30, Pallas kernels: none -> 88.8 us  [the longest x24 66.8 us: placed(): pl.pallas_call(place_kernel, grid_spec=pltpu.PrefetchScalarGridSpec(num_s...]
    unnamed x18 -> x25, local copies, waits for them, and re-layouts: 53.1 us -> 2.24 us
    all_gather x1, blocking collectives: 45 us -> 9.16 us  [body(): gain = lax.all_gather(gain, 'model', axis=0, tiled=True)]
    dot_general x4 -> x0, matrix products: 15.6 us -> none  [the longest x1 5.61 us: body(): jnp.dot(low_mixed, high_mixed, preferred_element_type=jnp.float32)]
    ppermute x0 -> x21, starting transfers between devices: none -> 14.8 us  [the longest x18 13.3 us: body(): arrived[number] = lax.ppermute(piece, 'rows', ring)]
  transfers between devices with their start and end apart: 4 -> 21, of which waited for: 3 -> 10; matrix products, arithmetic and copies ran while one was open for 6% -> 0% of each run, Pallas kernels for 0% -> 12%
where the time goes in v1:
time: 658 us; the launch traced here: 657 us
  waiting for transfers between devices  541 us (82%)
  Pallas kernels  88.8 us (13%)
  starting transfers between devices  14.8 us (2%)
  blocking collectives  9.16 us (1%)
    ppermute x18, waiting for transfers between devices, body(): arrived[number] = lax.ppermute(piece, 'rows', ring)  372 us
    ppermute x3, waiting for transfers between devices, body(): gain = lax.ppermute(gain, 'rows', ring)  168 us
    pallas_call x24, Pallas kernels, placed(): pl.pallas_call(place_kernel, grid_spec=pltpu.PrefetchScalarGridSpec(num_s...  66.8 us
    pallas_call x6, Pallas kernels, merged(): pl.pallas_call(merge_kernel, grid=(tiles,), in_specs=[pl.BlockSpec((depth...  22 us
    ppermute x18, starting transfers between devices, body(): arrived[number] = lax.ppermute(piece, 'rows', ring)  13.3 us
  transfers between devices with their start and end apart: 21, of which 10 were waited for; matrix products, arithmetic and copies ran while one was open for 0% of the time, Pallas kernels for 12%

profile of v1, /device:TPU:0, one launch (start us, length us, event | category | flops | bytes accessed | tf_op | source)
XLA Modules:
  0.0 656.8 jit_solution(11551327296135369277)
XLA Ops:
  5.1 4.4 merge.8.refs_0_
  12.5 4.4 merge.9.refs_1_
  18.5 4.4 merge.10.refs_0_
  24.4 4.4 merge.11.refs_1_
  28.9 3.8 place.26.refs_0_
  32.6 3.8 place.27.refs_0_
  36.4 24.9 %collective-permute-done.2.refs_1_ = bf16[512,2048]{1,0:T(8,128)(2,1)} collective-permute-done((bf16[512,2048]{1,0:T(8,128)(2,1)}, bf16[512,2048]{1,0:T(8,128)(2,1)}, u32[]{:S(2)}, u32[]{:S(2)}) %collective-permute-start.2) | collective-permute-done | bytes 2097184 | tf_op jit(solution)/shard_map/ppermute | solution.py:153
  69.1 37.1 %collective-permute-done.1.refs_1_ = bf16[512,2048]{1,0:T(8,128)(2,1)} collective-permute-done((bf16[512,2048]{1,0:T(8,128)(2,1)}, bf16[512,2048]{1,0:T(8,128)(2,1)}, u32[]{:S(2)}, u32[]{:S(2)}) %collective-permute-start.1) | collective-permute-done | bytes 2097184 | tf_op jit(solution)/shard_map/ppermute | solution.py:153
  108.9 42.3 %collective-permute-done.refs_1_ = bf16[1024,1024]{1,0:T(8,128)(2,1)} collective-permute-done((bf16[1024,1024]{1,0:T(8,128)(2,1)}, bf16[1024,1024]{1,0:T(8,128)(2,1)}, u32[]{:S(2)}, u32[]{:S(2)}) %collective-permute-start) | collective-permute-done | bytes 2097184 | tf_op jit(solution)/shard_map/ppermute | solution.py:153
  151.2 3.8 place.32.refs_0_
  155.0 41.1 %collective-permute-done.8.refs_1_ = bf16[1024,1024]{1,0:T(8,128)(2,1)} collective-permute-done((bf16[1024,1024]{1,0:T(8,128)(2,1)}, bf16[1024,1024]{1,0:T(8,128)(2,1)}, u32[]{:S(2)}, u32[]{:S(2)}) %collective-permute-start.8) | collective-permute-done | bytes 2097184 | tf_op jit(solution)/shard_map/ppermute | solution.py:153
  196.2 9.2 %all-gather = bf16[8,1,256]{2,1,0:T(2,128)(2,1)S(1)} all-gather(bf16[1,1,256]{2,1,0:T(2,128)(2,1)S(1)} %reshape.30), channel_id=1, replica_groups=mesh['rows'=4,'model'=8] {'model'}, dimensions={0}, use_global_device_ids=true | all-gather | bytes 4608 | tf_op jit(solution)/shard_map/all_gather | solution.py:133
  206.8 168.3 %collective-permute-done.18 = bf16[2048]{0:T(1024)(128)(2,1)S(1)} collective-permute-done((bf16[2048]{0:T(1024)(128)(2,1)S(1)}, bf16[2048]{0:T(1024)(128)(2,1)S(1)}, u32[]{:S(2)}, u32[]{:S(2)}) %collective-permute-start.18) | collective-permute-done | bytes 4128 | tf_op jit(solution)/shard_map/ppermute | solution.py:159
  375.1 14.9 %collective-permute-done.7.refs_1_ = bf16[128,2048]{1,0:T(8,128)(2,1)S(1)} collective-permute-done((bf16[128,2048]{1,0:T(8,128)(2,1)S(1)}, bf16[128,2048]{1,0:T(8,128)(2,1)S(1)}, u32[]{:S(2)}, u32[]{:S(2)}) %collective-permute-start.7) | collective-permute-done | bytes 524320 | tf_op jit(solution)/shard_map/ppermute | solution.py:153
  390.8 3.8 place.33.refs_0_
  394.6 10.3 %collective-permute-done.6.refs_1_ = bf16[128,2048]{1,0:T(8,128)(2,1)S(1)} collective-permute-done((bf16[128,2048]{1,0:T(8,128)(2,1)S(1)}, bf16[128,2048]{1,0:T(8,128)(2,1)S(1)}, u32[]{:S(2)}, u32[]{:S(2)}) %collective-permute-start.6) | collective-permute-done | bytes 524320 | tf_op jit(solution)/shard_map/ppermute | solution.py:153
  418.3 3.9 place.40.refs_0_
  422.2 4.2 collective-permute-start.17
  427.1 184.1 %collective-permute-done.11.refs_1_ = bf16[128,2048]{1,0:T(8,128)(2,1)S(1)} collective-permute-done((bf16[128,2048]{1,0:T(8,128)(2,1)}, bf16[128,2048]{1,0:T(8,128)(2,1)S(1)}, u32[]{:S(2)}, u32[]{:S(2)}) %collective-permute-start.11) | collective-permute-done | bytes 524320 | tf_op jit(solution)/shard_map/ppermute | solution.py:153
  611.3 4.0 place.41.refs_0_
  619.1 10.5 %collective-permute-done.15.refs_1_ = bf16[128,2048]{1,0:T(8,128)(2,1)} collective-permute-done((bf16[128,2048]{1,0:T(8,128)(2,1)S(1)}, bf16[128,2048]{1,0:T(8,128)(2,1)}, u32[]{:S(2)}, u32[]{:S(2)}) %collective-permute-start.15) | collective-permute-done | bytes 524320 | tf_op jit(solution)/shard_map/ppermute | solution.py:153
  634.4 6.9 %collective-permute-done.14.refs_1_ = bf16[128,2048]{1,0:T(8,128)(2,1)S(1)} collective-permute-done((bf16[128,2048]{1,0:T(8,128)(2,1)}, bf16[128,2048]{1,0:T(8,128)(2,1)S(1)}, u32[]{:S(2)}, u32[]{:S(2)}) %collective-permute-start.14) | collective-permute-done | bytes 524320 | tf_op jit(solution)/shard_map/ppermute | solution.py:153
  644.0 3.8 place.46.refs_0_
  647.8 3.8 place.47
  (84 shorter events, 54.0 us)
Async XLA Ops:
  9.4 51.9 %collective-permute-start.2 = (bf16[512,2048]{1,0:T(8,128)(2,1)}, bf16[512,2048]{1,0:T(8,128)(2,1)}, u32[]{:S(2)}, u32[]{:S(2)}) collective-permute-start(bf16[512,2048]{1,0:T(8,128)(2,1)} %merge.8.refs_0_), channel_id=1, source_target_pairs={{0,8},{8,16},{16,24},{24,0},{1,9},{9,17},{17,25},{25,1},{2,10},{10... | collective-permute-start | bytes 6291464 | tf_op jit(solution)/shard_map/ppermute | solution.py:153
  16.9 89.4 %collective-permute-start.1 = (bf16[512,2048]{1,0:T(8,128)(2,1)}, bf16[512,2048]{1,0:T(8,128)(2,1)}, u32[]{:S(2)}, u32[]{:S(2)}) collective-permute-start(bf16[512,2048]{1,0:T(8,128)(2,1)} %merge.9.refs_1_), channel_id=1, source_target_pairs={{0,8},{8,16},{16,24},{24,0},{1,9},{9,17},{17,25},{25,1},{2,10},{10... | collective-permute-start | bytes 6291464 | tf_op jit(solution)/shard_map/ppermute | solution.py:153
  22.9 128.3 %collective-permute-start = (bf16[1024,1024]{1,0:T(8,128)(2,1)}, bf16[1024,1024]{1,0:T(8,128)(2,1)}, u32[]{:S(2)}, u32[]{:S(2)}) collective-permute-start(bf16[1024,1024]{1,0:T(8,128)(2,1)} %merge.10.refs_0_), channel_id=1, source_target_pairs={{0,8},{8,16},{16,24},{24,0},{1,9},{9,17},{17,25},{25,1},{2,10},{10... | collective-permute-start | bytes 6291464 | tf_op jit(solution)/shard_map/ppermute | solution.py:153
  28.9 167.3 %collective-permute-start.8 = (bf16[1024,1024]{1,0:T(8,128)(2,1)}, bf16[1024,1024]{1,0:T(8,128)(2,1)}, u32[]{:S(2)}, u32[]{:S(2)}) collective-permute-start(bf16[1024,1024]{1,0:T(8,128)(2,1)} %merge.11.refs_1_), channel_id=1, source_target_pairs={{0,8},{8,16},{16,24},{24,0},{1,9},{9,17},{17,25},{25,1},{2,10},{10... | collective-permute-start | bytes 6291464 | tf_op jit(solution)/shard_map/ppermute | solution.py:153
  61.3 343.6 %collective-permute-start.5 = (bf16[512,2048]{1,0:T(8,128)(2,1)}, bf16[512,2048]{1,0:T(8,128)(2,1)S(1)}, u32[]{:S(2)}, u32[]{:S(2)}) collective-permute-start(bf16[512,2048]{1,0:T(8,128)(2,1)} %collective-permute-done.2.refs_1_), channel_id=1, source_target_pairs={{0,8},{8,16},{16,24},{24,0},{1,9},{9,17},{17,25},{25,1},{2,10},{10... | collective-permute-start | bytes 6291464 | tf_op jit(solution)/shard_map/ppermute | solution.py:153
  106.3 309.2 %collective-permute-start.4 = (bf16[512,2048]{1,0:T(8,128)(2,1)}, bf16[512,2048]{1,0:T(8,128)(2,1)}, u32[]{:S(2)}, u32[]{:S(2)}) collective-permute-start(bf16[512,2048]{1,0:T(8,128)(2,1)} %collective-permute-done.1.refs_1_), channel_id=1, source_target_pairs={{0,8},{8,16},{16,24},{24,0},{1,9},{9,17},{17,25},{25,1},{2,10},{10... | collective-permute-start | bytes 6291464 | tf_op jit(solution)/shard_map/ppermute | solution.py:153
  108.9 266.2 %copy-start.3 = (bf16[128,2048]{1,0:T(8,128)(2,1)S(1)}, bf16[128,2048]{1,0:T(8,128)(2,1)}, u32[]{:S(2)}) copy-start(bf16[128,2048]{1,0:T(8,128)(2,1)} %merge.6.refs_0_) | copy-start | bytes 1572868
  108.9 281.9 %copy-start.2 = (bf16[128,2048]{1,0:T(8,128)(2,1)S(1)}, bf16[128,2048]{1,0:T(8,128)(2,1)}, u32[]{:S(2)}) copy-start(bf16[128,2048]{1,0:T(8,128)(2,1)} %merge.7.refs_0_) | copy-start | bytes 1572868
  151.2 266.9 %collective-permute-start.3 = (bf16[1024,1024]{1,0:T(8,128)(2,1)}, bf16[1024,1024]{1,0:T(8,128)(2,1)}, u32[]{:S(2)}, u32[]{:S(2)}) collective-permute-start(bf16[1024,1024]{1,0:T(8,128)(2,1)} %collective-permute-done.refs_1_), channel_id=1, source_target_pairs={{0,8},{8,16},{16,24},{24,0},{1,9},{9,17},{17,25},{25,1},{2,10},{10... | collective-permute-start | bytes 6291464 | tf_op jit(solution)/shard_map/ppermute | solution.py:153
  196.1 226.0 %collective-permute-start.13 = (bf16[1024,1024]{1,0:T(8,128)(2,1)}, bf16[1024,1024]{1,0:T(8,128)(2,1)}, u32[]{:S(2)}, u32[]{:S(2)}) collective-permute-start(bf16[1024,1024]{1,0:T(8,128)(2,1)} %collective-permute-done.8.refs_1_), channel_id=1, source_target_pairs={{0,8},{8,16},{16,24},{24,0},{1,9},{9,17},{17,25},{25,1},{2,10},{10... | collective-permute-start | bytes 6291464 | tf_op jit(solution)/shard_map/ppermute | solution.py:153
  205.4 169.7 %collective-permute-start.18 = (bf16[2048]{0:T(1024)(128)(2,1)S(1)}, bf16[2048]{0:T(1024)(128)(2,1)S(1)}, u32[]{:S(2)}, u32[]{:S(2)}) collective-permute-start(bf16[2048]{0:T(1024)(128)(2,1)S(1)} %bitcast.23), channel_id=1, source_target_pairs={{0,8},{8,16},{16,24},{24,0},{1,9},{9,17},{17,25},{25,1},{2,10},{10... | collective-permute-start | bytes 12296 | tf_op jit(solution)/shard_map/ppermute | solution.py:159
  375.1 14.9 %collective-permute-start.7 = (bf16[128,2048]{1,0:T(8,128)(2,1)S(1)}, bf16[128,2048]{1,0:T(8,128)(2,1)S(1)}, u32[]{:S(2)}, u32[]{:S(2)}) collective-permute-start(bf16[128,2048]{1,0:T(8,128)(2,1)S(1)} %copy-done.3), channel_id=1, source_target_pairs={{0,8},{8,16},{16,24},{24,0},{1,9},{9,17},{17,25},{25,1},{2,10},{10... | collective-permute-start | bytes 1572872 | tf_op jit(solution)/shard_map/ppermute | solution.py:153
  390.8 14.1 %collective-permute-start.6 = (bf16[128,2048]{1,0:T(8,128)(2,1)S(1)}, bf16[128,2048]{1,0:T(8,128)(2,1)S(1)}, u32[]{:S(2)}, u32[]{:S(2)}) collective-permute-start(bf16[128,2048]{1,0:T(8,128)(2,1)S(1)} %copy-done.2), channel_id=1, source_target_pairs={{0,8},{8,16},{16,24},{24,0},{1,9},{9,17},{17,25},{25,1},{2,10},{10... | collective-permute-start | bytes 1572872 | tf_op jit(solution)/shard_map/ppermute | solution.py:153
  404.9 22.1 %collective-permute-start.12 = (bf16[128,2048]{1,0:T(8,128)(2,1)}, bf16[128,2048]{1,0:T(8,128)(2,1)S(1)}, u32[]{:S(2)}, u32[]{:S(2)}) collective-permute-start(bf16[128,2048]{1,0:T(8,128)(2,1)} %copy-done.7), channel_id=1, source_target_pairs={{0,8},{8,16},{16,24},{24,0},{1,9},{9,17},{17,25},{25,1},{2,10},{10... | collective-permute-start | bytes 1572872 | tf_op jit(solution)/shard_map/ppermute | solution.py:153
  404.9 22.1 %collective-permute-start.19 = (bf16[2048]{0:T(1024)(128)(2,1)S(1)}, bf16[2048]{0:T(1024)(128)(2,1)S(1)}, u32[]{:S(2)}, u32[]{:S(2)}) collective-permute-start(bf16[2048]{0:T(1024)(128)(2,1)S(1)} %collective-permute-done.18), channel_id=1, source_target_pairs={{0,8},{8,16},{16,24},{24,0},{1,9},{9,17},{17,25},{25,1},{2,10},{10... | collective-permute-start | bytes 12296 | tf_op jit(solution)/shard_map/ppermute | solution.py:159
  418.1 225.9 %collective-permute-start.16 = (bf16[1024,1024]{1,0:T(8,128)(2,1)}, bf16[1024,1024]{1,0:T(8,128)(2,1)}, u32[]{:S(2)}, u32[]{:S(2)}) collective-permute-start(bf16[1024,1024]{1,0:T(8,128)(2,1)} %collective-permute-done.3.refs_1_), channel_id=1, source_target_pairs={{0,8},{8,16},{16,24},{24,0},{1,9},{9,17},{17,25},{25,1},{2,10},{10... | collective-permute-start | bytes 6291464 | tf_op jit(solution)/shard_map/ppermute | solution.py:153
  422.2 225.6 %collective-permute-start.17 = (bf16[1024,1024]{1,0:T(8,128)(2,1)}, bf16[1024,1024]{1,0:T(8,128)(2,1)}, u32[]{:S(2)}, u32[]{:S(2)}) collective-permute-start(bf16[1024,1024]{1,0:T(8,128)(2,1)} %collective-permute-done.13.refs_1_), channel_id=1, source_target_pairs={{0,8},{8,16},{16,24},{24,0},{1,9},{9,17},{17,25},{25,1},{2,10},{10... | collective-permute-start | bytes 6291464 | tf_op jit(solution)/shard_map/ppermute | solution.py:153
  426.4 225.2 %collective-permute-start.9 = (bf16[512,2048]{1,0:T(8,128)(2,1)S(1)}, bf16[512,2048]{1,0:T(8,128)(2,1)}, u32[]{:S(2)}, u32[]{:S(2)}) collective-permute-start(bf16[512,2048]{1,0:T(8,128)(2,1)S(1)} %copy-done.1), channel_id=1, source_target_pairs={{0,8},{8,16},{16,24},{24,0},{1,9},{9,17},{17,25},{25,1},{2,10},{10... | collective-permute-start | bytes 6291464 | tf_op jit(solution)/shard_map/ppermute | solution.py:153
  427.0 227.2 %collective-permute-start.10 = (bf16[512,2048]{1,0:T(8,128)(2,1)}, bf16[512,2048]{1,0:T(8,128)(2,1)}, u32[]{:S(2)}, u32[]{:S(2)}) collective-permute-start(bf16[512,2048]{1,0:T(8,128)(2,1)} %collective-permute-done.4.refs_1_), channel_id=1, source_target_pairs={{0,8},{8,16},{16,24},{24,0},{1,9},{9,17},{17,25},{25,1},{2,10},{10... | collective-permute-start | bytes 6291464 | tf_op jit(solution)/shard_map/ppermute | solution.py:153
  427.0 188.2 %copy-start.4 = (bf16[128,2048]{1,0:T(8,128)(2,1)}, bf16[128,2048]{1,0:T(8,128)(2,1)S(1)}, u32[]{:S(2)}) copy-start(bf16[128,2048]{1,0:T(8,128)(2,1)S(1)} %collective-permute-done.12.refs_1_) | copy-start | bytes 1572868
  427.0 184.2 %collective-permute-start.11 = (bf16[128,2048]{1,0:T(8,128)(2,1)}, bf16[128,2048]{1,0:T(8,128)(2,1)S(1)}, u32[]{:S(2)}, u32[]{:S(2)}) collective-permute-start(bf16[128,2048]{1,0:T(8,128)(2,1)} %copy-done.6), channel_id=1, source_target_pairs={{0,8},{8,16},{16,24},{24,0},{1,9},{9,17},{17,25},{25,1},{2,10},{10... | collective-permute-start | bytes 1572872 | tf_op jit(solution)/shard_map/ppermute | solution.py:153
  611.3 5.9 collective-permute-start.20
  617.1 12.5 %collective-permute-start.15 = (bf16[128,2048]{1,0:T(8,128)(2,1)S(1)}, bf16[128,2048]{1,0:T(8,128)(2,1)}, u32[]{:S(2)}, u32[]{:S(2)}) collective-permute-start(bf16[128,2048]{1,0:T(8,128)(2,1)S(1)} %collective-permute-done.11.refs_1_), channel_id=1, source_target_pairs={{0,8},{8,16},{16,24},{24,0},{1,9},{9,17},{17,25},{25,1},{2,10},{10... | collective-permute-start | bytes 1572872 | tf_op jit(solution)/shard_map/ppermute | solution.py:153
  629.6 11.7 %collective-permute-start.14 = (bf16[128,2048]{1,0:T(8,128)(2,1)}, bf16[128,2048]{1,0:T(8,128)(2,1)S(1)}, u32[]{:S(2)}, u32[]{:S(2)}) collective-permute-start(bf16[128,2048]{1,0:T(8,128)(2,1)} %copy-done.4), channel_id=1, source_target_pairs={{0,8},{8,16},{16,24},{24,0},{1,9},{9,17},{17,25},{25,1},{2,10},{10... | collective-permute-start | bytes 1572872 | tf_op jit(solution)/shard_map/ppermute | solution.py:153
  (8 other events, 198.7 us)

commit v2 on v1

--- a/solution.py
+++ b/solution.py
@@ -17,42 +17,50 @@
     out_ref[...] = whole.astype(out_ref.dtype)
 
 
-def merged(train, low, high, part, parts):
+def merged(train, low, high, cut, part, parts):
     depth, width = train.shape
-    rank = low.shape[1]
-    tile = min(256 if depth <= 1024 else 128, width // parts)
-    tiles = width // parts // tile
+    rank = low.shape[0]
+    if cut == 0:
+        width = width // parts
+        tile = min(256 if depth <= 1024 else 128, width)
+        tiles, first, across = width // tile, part * (width // tile), 0
+    else:
+        depth = depth // parts
+        tile = width
+        tiles, first, across = 1, 0, part
     return pl.pallas_call(
         merge_kernel,
         grid=(tiles,),
         in_specs=[
-            pl.BlockSpec((depth, tile), lambda i: (0, part * tiles + i)),
-            pl.BlockSpec((rank, depth), lambda i: (0, 0)),
-            pl.BlockSpec((rank, tile), lambda i: (0, part * tiles + i)),
+            pl.BlockSpec((depth, tile), lambda i: (across, first + i)),
+            pl.BlockSpec((rank, depth), lambda i: (0, across)),
+            pl.BlockSpec((rank, tile), lambda i: (0, first + i)),
         ],
         out_specs=pl.BlockSpec((tile, depth), lambda i: (i, 0)),
-        out_shape=jax.ShapeDtypeStruct((width // parts, depth), train.dtype),
+        out_shape=jax.ShapeDtypeStruct((width, depth), train.dtype),
         cost_estimate=pl.CostEstimate(
-            flops=2 * rank * depth * width // parts,
-            bytes_accessed=4 * depth * width // parts,
+            flops=2 * rank * depth * width,
+            bytes_accessed=4 * depth * width,
             transcendentals=0,
         ),
         name="merge",
-    )(train, low.T, high)
+    )(train, low, high)
 
 
 def place_kernel(owner_ref, *refs):
     refs[-1][...] = refs[-2][...]
 
 
-def placed(whole, piece, owner, shape, axis, part, parts):
+def placed(whole, piece, owner, shape, axis, cut, part, parts):
     rows, width = piece.shape
     tile = min(rows, 256)
     tiles = rows // tile
-    if axis == 1:
+    if axis == 0:
+        spot = lambda i, owner: ((owner[0] * parts + part) * tiles + i, 0)
+    elif cut == 0:
         spot = lambda i, owner: (part * tiles + i, owner[0])
     else:
-        spot = lambda i, owner: ((owner[0] * parts + part) * tiles + i, 0)
+        spot = lambda i, owner: (i, owner[0] * parts + part)
     before = [] if whole is None else [whole]
     return pl.pallas_call(
         place_kernel,
@@ -76,8 +84,20 @@
     return lax.optimization_barrier((value, earlier))
 
 
-def order(step, count):
-    return list(range(count)) if step == 1 else list(range(2, count)) + [0, 1]
+plan = [
+    ("key", 0, 0, 1),
+    ("value", 0, 0, 1),
+    ("query", 0, 0, 2),
+    ("query", 0, 1, 2),
+    ("mixed", 0, 0, 2),
+    ("mixed", 0, 1, 2),
+]
+small = 2
+
+
+def order(step):
+    count = len(plan)
+    return list(range(count)) if step == 1 else list(range(small, count)) + list(range(small))
 
 
 def body(
@@ -107,14 +127,6 @@
         "query": (train_query, low_query, high_query, 1),
         "mixed": (train_mixed, low_mixed, high_mixed, 0),
     }
-    plan = [
-        ("key", 0, 1),
-        ("value", 0, 1),
-        ("query", 0, 2),
-        ("query", 1, 2),
-        ("mixed", 0, 2),
-        ("mixed", 1, 2),
-    ]
     shapes, outs = {}, {}
     for name, (train, _, _, axis) in weights.items():
         shape = [train.shape[1], train.shape[0]]
@@ -123,28 +135,37 @@
         outs[name] = None
 
     def place(number, piece, step):
-        name, part, parts = plan[number]
+        name, cut, part, parts = plan[number]
+        axis = weights[name][3]
         outs[name] = placed(
-            outs[name], piece, owners[step], shapes[name], weights[name][3], part, parts
+            outs[name], piece, owners[step], shapes[name], axis, cut, part, parts
         )
         return name
 
     gain = (norm_train + norm_step).astype(jnp.bfloat16)
     gain = lax.all_gather(gain, "model", axis=0, tiled=True)
 
-    own = []
-    for name, part, parts in plan:
+    own, previous = {}, None
+    for number in list(range(1, len(plan))) + [0]:
+        name, cut, part, parts = plan[number]
         train, low, high, _ = weights[name]
-        if own:
-            high, own[-1] = after(high, own[-1])
-        own.append(merged(train, low, high, part, parts))
-    moving = list(own)
+        if previous is not None:
+            high, own[previous] = after(high, own[previous])
+        own[number] = merged(train, low.T, high, cut, part, parts)
+        previous = number
+    moving = [own[number] for number in range(len(plan))]
+    moving[0] = train_key
+    share = low_key.shape[0] // lax.axis_size("model")
+    low_share = lax.dynamic_slice_in_dim(
+        low_key.T, lax.axis_index("model") * share, share, 1
+    )
+    low_share = lax.ppermute(low_share, "rows", ring)
     serve_norm = lax.dynamic_update_slice_in_dim(
         jnp.zeros((n, gain.shape[0]), gain.dtype), gain[None], me, 0
     )
     last = None
     for step in range(1, n):
-        turn = order(step, len(plan))
+        turn = order(step)
         arrived = {}
         for number in turn:
             piece = moving[number]
@@ -154,6 +175,8 @@
             if step > 1:
                 last = place(number, piece, step - 1)
         if step == 1:
+            low_moved = lax.all_gather(low_share, "model", axis=1, tiled=True)
+            arrived[0] = merged(arrived[0], low_moved, high_key, *plan[0][1:])
             for number in turn:
                 last = place(number, own[number], 0)
         gain = lax.ppermute(gain, "rows", ring)
@@ -161,7 +184,7 @@
             serve_norm, gain[None], owners[step][0], 0
         )
         moving = [arrived[number] for number in range(len(plan))]
-    for number in order(n - 1, len(plan)):
+    for number in order(n - 1):
         place(number, moving[number], n - 1)
     serve_norm = jnp.reshape(serve_norm, (-1,))
     return (outs["query"], outs["key"], outs["value"], outs["mixed"], serve_norm)

time: 658 us -> 672 us (1.021)
  blocking collectives: 9.16 us -> 19 us
    all_gather x0 -> x1, blocking collectives: none -> 9.86 us  [body(): low_moved = lax.all_gather(low_share, 'model', axis=1, tiled=True)]
    ppermute x18, waiting for transfers between devices: 372 us -> 365 us  [body(): arrived[number] = lax.ppermute(piece, 'rows', ring)]
    pallas_call x6 -> x7, Pallas kernels: 22 us -> 24.2 us  [merged(): pl.pallas_call(merge_kernel, grid=(tiles,), in_specs=[pl.BlockSpec((depth...]
  transfers between devices with their start and end apart: 21 -> 22, of which waited for: 10 -> 10; matrix products, arithmetic and copies ran while one was open for 0% -> 0% of each run, Pallas kernels for 12% -> 12%
where the time goes in v2:
time: 672 us; the launch traced here: 671 us
  waiting for transfers between devices  538 us (80%)
  Pallas kernels  90.8 us (14%)
  blocking collectives  19 us (3%)
  starting transfers between devices  18.7 us (3%)
    ppermute x18, waiting for transfers between devices, body(): arrived[number] = lax.ppermute(piece, 'rows', ring)  365 us
    ppermute x3, waiting for transfers between devices, body(): gain = lax.ppermute(gain, 'rows', ring)  168 us
    pallas_call x24, Pallas kernels, placed(): pl.pallas_call(place_kernel, grid_spec=pltpu.PrefetchScalarGridSpec(num_s...  66.6 us
    pallas_call x7, Pallas kernels, merged(): pl.pallas_call(merge_kernel, grid=(tiles,), in_specs=[pl.BlockSpec((depth...  24.2 us
    ppermute x18, starting transfers between devices, body(): arrived[number] = lax.ppermute(piece, 'rows', ring)  15.9 us
  transfers between devices with their start and end apart: 22, of which 10 were waited for; matrix products, arithmetic and copies ran while one was open for 0% of the time, Pallas kernels for 12%

profile of v2, /device:TPU:0, one launch (start us, length us, event | category | flops | bytes accessed | tf_op | source)
XLA Modules:
  0.0 670.5 jit_solution(768745263760126596)
XLA Ops:
  2.8 4.4 merge.8.refs_0_
  10.3 4.4 merge.9.refs_1_
  16.2 4.4 merge.10.refs_0_
  22.2 4.4 merge.11.refs_1_
  26.7 3.8 place.26.refs_0_
  30.4 3.8 place.27.refs_0_
  34.2 24.9 %collective-permute-done.2.refs_1_ = bf16[512,2048]{1,0:T(8,128)(2,1)} collective-permute-done((bf16[512,2048]{1,0:T(8,128)(2,1)}, bf16[512,2048]{1,0:T(8,128)(2,1)}, u32[]{:S(2)}, u32[]{:S(2)}) %collective-permute-start.2) | collective-permute-done | bytes 2097184 | tf_op jit(solution)/shard_map/ppermute | solution.py:174
  66.9 37.1 %collective-permute-done.1.refs_1_ = bf16[512,2048]{1,0:T(8,128)(2,1)} collective-permute-done((bf16[512,2048]{1,0:T(8,128)(2,1)}, bf16[512,2048]{1,0:T(8,128)(2,1)}, u32[]{:S(2)}, u32[]{:S(2)}) %collective-permute-start.1) | collective-permute-done | bytes 2097184 | tf_op jit(solution)/shard_map/ppermute | solution.py:174
  106.7 42.3 %collective-permute-done.refs_1_ = bf16[1024,1024]{1,0:T(8,128)(2,1)} collective-permute-done((bf16[1024,1024]{1,0:T(8,128)(2,1)}, bf16[1024,1024]{1,0:T(8,128)(2,1)}, u32[]{:S(2)}, u32[]{:S(2)}) %collective-permute-start) | collective-permute-done | bytes 2097184 | tf_op jit(solution)/shard_map/ppermute | solution.py:174
  149.0 3.8 place.32.refs_0_
  152.8 41.1 %collective-permute-done.9.refs_1_ = bf16[1024,1024]{1,0:T(8,128)(2,1)} collective-permute-done((bf16[1024,1024]{1,0:T(8,128)(2,1)}, bf16[1024,1024]{1,0:T(8,128)(2,1)}, u32[]{:S(2)}, u32[]{:S(2)}) %collective-permute-start.9) | collective-permute-done | bytes 2097184 | tf_op jit(solution)/shard_map/ppermute | solution.py:174
  194.0 9.2 %all-gather = bf16[8,1,256]{2,1,0:T(2,128)(2,1)S(1)} all-gather(bf16[1,1,256]{2,1,0:T(2,128)(2,1)S(1)} %reshape.30), channel_id=1, replica_groups=mesh['rows'=4,'model'=8] {'model'}, dimensions={0}, use_global_device_ids=true | all-gather | bytes 4608 | tf_op jit(solution)/shard_map/all_gather | solution.py:146
  205.3 167.6 %collective-permute-done.19 = bf16[2048]{0:T(1024)(128)(2,1)S(1)} collective-permute-done((bf16[2048]{0:T(1024)(128)(2,1)S(1)}, bf16[2048]{0:T(1024)(128)(2,1)S(1)}, u32[]{:S(2)}, u32[]{:S(2)}) %collective-permute-start.19) | collective-permute-done | bytes 4128 | tf_op jit(solution)/shard_map/ppermute | solution.py:182
  372.9 5.4 collective-permute-done.8
  378.3 13.8 %collective-permute-done.7.train_ref = bf16[2048,128]{1,0:T(8,128)(2,1)S(1)} collective-permute-done((bf16[2048,128]{1,0:T(8,128)(2,1)S(1)}, bf16[2048,128]{1,0:T(8,128)(2,1)S(1)}, u32[]{:S(2)}, u32[]{:S(2)}) %collective-permute-start.7) | collective-permute-done | bytes 524320 | tf_op jit(solution)/shard_map/ppermute | solution.py:174
  392.9 9.9 %all_gather.6.low_ref = bf16[16,2048]{1,0:T(8,128)(2,1)} all-gather(bf16[16,256]{1,0:T(8,128)(2,1)S(1)} %collective-permute-done.8), channel_id=1, replica_groups=mesh['rows'=4,'model'=8] {'model'}, dimensions={1}, use_global_device_ids=true | all-gather | bytes 73728 | tf_op jit(solution)/shard_map/all_gather | solution.py:178
  405.0 3.8 place.33.refs_0_
  427.9 3.8 place.40.refs_0_
  436.7 183.5 %collective-permute-done.12.refs_1_ = bf16[128,2048]{1,0:T(8,128)(2,1)S(1)} collective-permute-done((bf16[128,2048]{1,0:T(8,128)(2,1)}, bf16[128,2048]{1,0:T(8,128)(2,1)S(1)}, u32[]{:S(2)}, u32[]{:S(2)}) %collective-permute-start.12) | collective-permute-done | bytes 524320 | tf_op jit(solution)/shard_map/ppermute | solution.py:174
  621.5 3.8 place.41.refs_0_
  628.2 13.3 %collective-permute-done.16.refs_1_ = bf16[128,2048]{1,0:T(8,128)(2,1)S(1)} collective-permute-done((bf16[128,2048]{1,0:T(8,128)(2,1)S(1)}, bf16[128,2048]{1,0:T(8,128)(2,1)S(1)}, u32[]{:S(2)}, u32[]{:S(2)}) %collective-permute-start.16) | collective-permute-done | bytes 524320 | tf_op jit(solution)/shard_map/ppermute | solution.py:174
  646.2 8.9 %collective-permute-done.15.refs_1_ = bf16[128,2048]{1,0:T(8,128)(2,1)S(1)} collective-permute-done((bf16[128,2048]{1,0:T(8,128)(2,1)}, bf16[128,2048]{1,0:T(8,128)(2,1)S(1)}, u32[]{:S(2)}, u32[]{:S(2)}) %collective-permute-start.15) | collective-permute-done | bytes 524320 | tf_op jit(solution)/shard_map/ppermute | solution.py:174
  657.8 3.8 place.46.refs_0_
  661.5 3.8 place.47
  (91 shorter events, 64.9 us)
Async XLA Ops:
  7.2 51.9 %collective-permute-start.2 = (bf16[512,2048]{1,0:T(8,128)(2,1)}, bf16[512,2048]{1,0:T(8,128)(2,1)}, u32[]{:S(2)}, u32[]{:S(2)}) collective-permute-start(bf16[512,2048]{1,0:T(8,128)(2,1)} %merge.8.refs_0_), channel_id=1, source_target_pairs={{0,8},{8,16},{16,24},{24,0},{1,9},{9,17},{17,25},{25,1},{2,10},{10... | collective-permute-start | bytes 6291464 | tf_op jit(solution)/shard_map/ppermute | solution.py:174
  14.7 89.4 %collective-permute-start.1 = (bf16[512,2048]{1,0:T(8,128)(2,1)}, bf16[512,2048]{1,0:T(8,128)(2,1)}, u32[]{:S(2)}, u32[]{:S(2)}) collective-permute-start(bf16[512,2048]{1,0:T(8,128)(2,1)} %merge.9.refs_1_), channel_id=1, source_target_pairs={{0,8},{8,16},{16,24},{24,0},{1,9},{9,17},{17,25},{25,1},{2,10},{10... | collective-permute-start | bytes 6291464 | tf_op jit(solution)/shard_map/ppermute | solution.py:174
  20.7 128.3 %collective-permute-start = (bf16[1024,1024]{1,0:T(8,128)(2,1)}, bf16[1024,1024]{1,0:T(8,128)(2,1)}, u32[]{:S(2)}, u32[]{:S(2)}) collective-permute-start(bf16[1024,1024]{1,0:T(8,128)(2,1)} %merge.10.refs_0_), channel_id=1, source_target_pairs={{0,8},{8,16},{16,24},{24,0},{1,9},{9,17},{17,25},{25,1},{2,10},{10... | collective-permute-start | bytes 6291464 | tf_op jit(solution)/shard_map/ppermute | solution.py:174
  26.6 167.3 %collective-permute-start.9 = (bf16[1024,1024]{1,0:T(8,128)(2,1)}, bf16[1024,1024]{1,0:T(8,128)(2,1)}, u32[]{:S(2)}, u32[]{:S(2)}) collective-permute-start(bf16[1024,1024]{1,0:T(8,128)(2,1)} %merge.11.refs_1_), channel_id=1, source_target_pairs={{0,8},{8,16},{16,24},{24,0},{1,9},{9,17},{17,25},{25,1},{2,10},{10... | collective-permute-start | bytes 6291464 | tf_op jit(solution)/shard_map/ppermute | solution.py:174
  59.1 349.7 %collective-permute-start.5 = (bf16[512,2048]{1,0:T(8,128)(2,1)}, bf16[512,2048]{1,0:T(8,128)(2,1)S(1)}, u32[]{:S(2)}, u32[]{:S(2)}) collective-permute-start(bf16[512,2048]{1,0:T(8,128)(2,1)} %collective-permute-done.2.refs_1_), channel_id=1, source_target_pairs={{0,8},{8,16},{16,24},{24,0},{1,9},{9,17},{17,25},{25,1},{2,10},{10... | collective-permute-start | bytes 6291464 | tf_op jit(solution)/shard_map/ppermute | solution.py:174
  104.0 317.6 %collective-permute-start.4 = (bf16[512,2048]{1,0:T(8,128)(2,1)}, bf16[512,2048]{1,0:T(8,128)(2,1)}, u32[]{:S(2)}, u32[]{:S(2)}) collective-permute-start(bf16[512,2048]{1,0:T(8,128)(2,1)} %collective-permute-done.1.refs_1_), channel_id=1, source_target_pairs={{0,8},{8,16},{16,24},{24,0},{1,9},{9,17},{17,25},{25,1},{2,10},{10... | collective-permute-start | bytes 6291464 | tf_op jit(solution)/shard_map/ppermute | solution.py:174
  106.7 271.6 %copy-start.8 = (bf16[2048,128]{1,0:T(8,128)(2,1)S(1)}, bf16[2048,128]{1,0:T(8,128)(2,1)}, u32[]{:S(2)}) copy-start(bf16[2048,128]{1,0:T(8,128)(2,1)} %train_ref.11) | copy-start | bytes 1572868
  106.7 285.4 %copy-start.3 = (bf16[128,2048]{1,0:T(8,128)(2,1)S(1)}, bf16[128,2048]{1,0:T(8,128)(2,1)}, u32[]{:S(2)}) copy-start(bf16[128,2048]{1,0:T(8,128)(2,1)} %merge.7.refs_0_) | copy-start | bytes 1572868
  149.0 275.2 %collective-permute-start.3 = (bf16[1024,1024]{1,0:T(8,128)(2,1)}, bf16[1024,1024]{1,0:T(8,128)(2,1)}, u32[]{:S(2)}, u32[]{:S(2)}) collective-permute-start(bf16[1024,1024]{1,0:T(8,128)(2,1)} %collective-permute-done.refs_1_), channel_id=1, source_target_pairs={{0,8},{8,16},{16,24},{24,0},{1,9},{9,17},{17,25},{25,1},{2,10},{10... | collective-permute-start | bytes 6291464 | tf_op jit(solution)/shard_map/ppermute | solution.py:174
  193.9 237.8 %collective-permute-start.14 = (bf16[1024,1024]{1,0:T(8,128)(2,1)}, bf16[1024,1024]{1,0:T(8,128)(2,1)}, u32[]{:S(2)}, u32[]{:S(2)}) collective-permute-start(bf16[1024,1024]{1,0:T(8,128)(2,1)} %collective-permute-done.9.refs_1_), channel_id=1, source_target_pairs={{0,8},{8,16},{16,24},{24,0},{1,9},{9,17},{17,25},{25,1},{2,10},{10... | collective-permute-start | bytes 6291464 | tf_op jit(solution)/shard_map/ppermute | solution.py:174
  203.2 169.7 %collective-permute-start.19 = (bf16[2048]{0:T(1024)(128)(2,1)S(1)}, bf16[2048]{0:T(1024)(128)(2,1)S(1)}, u32[]{:S(2)}, u32[]{:S(2)}) collective-permute-start(bf16[2048]{0:T(1024)(128)(2,1)S(1)} %bitcast.25), channel_id=1, source_target_pairs={{0,8},{8,16},{16,24},{24,0},{1,9},{9,17},{17,25},{25,1},{2,10},{10... | collective-permute-start | bytes 12296 | tf_op jit(solution)/shard_map/ppermute | solution.py:182
  372.9 5.4 collective-permute-start.8
  378.3 13.8 %collective-permute-start.7 = (bf16[2048,128]{1,0:T(8,128)(2,1)S(1)}, bf16[2048,128]{1,0:T(8,128)(2,1)S(1)}, u32[]{:S(2)}, u32[]{:S(2)}) collective-permute-start(bf16[2048,128]{1,0:T(8,128)(2,1)S(1)} %copy-done.8), channel_id=1, source_target_pairs={{0,8},{8,16},{16,24},{24,0},{1,9},{9,17},{17,25},{25,1},{2,10},{10... | collective-permute-start | bytes 1572872 | tf_op jit(solution)/shard_map/ppermute | solution.py:174
  392.1 16.7 %collective-permute-start.6 = (bf16[128,2048]{1,0:T(8,128)(2,1)S(1)}, bf16[128,2048]{1,0:T(8,128)(2,1)}, u32[]{:S(2)}, u32[]{:S(2)}) collective-permute-start(bf16[128,2048]{1,0:T(8,128)(2,1)S(1)} %copy-done.3), channel_id=1, source_target_pairs={{0,8},{8,16},{16,24},{24,0},{1,9},{9,17},{17,25},{25,1},{2,10},{10... | collective-permute-start | bytes 1572872 | tf_op jit(solution)/shard_map/ppermute | solution.py:174
  408.8 24.3 %collective-permute-start.13 = (bf16[128,2048]{1,0:T(8,128)(2,1)S(1)}, bf16[128,2048]{1,0:T(8,128)(2,1)S(1)}, u32[]{:S(2)}, u32[]{:S(2)}) collective-permute-start(bf16[128,2048]{1,0:T(8,128)(2,1)S(1)} %copy-done.2), channel_id=1, source_target_pairs={{0,8},{8,16},{16,24},{24,0},{1,9},{9,17},{17,25},{25,1},{2,10},{10... | collective-permute-start | bytes 1572872 | tf_op jit(solution)/shard_map/ppermute | solution.py:174
  408.9 24.2 %collective-permute-start.20 = (bf16[2048]{0:T(1024)(128)(2,1)S(1)}, bf16[2048]{0:T(1024)(128)(2,1)S(1)}, u32[]{:S(2)}, u32[]{:S(2)}) collective-permute-start(bf16[2048]{0:T(1024)(128)(2,1)S(1)} %collective-permute-done.19), channel_id=1, source_target_pairs={{0,8},{8,16},{16,24},{24,0},{1,9},{9,17},{17,25},{25,1},{2,10},{10... | collective-permute-start | bytes 12296 | tf_op jit(solution)/shard_map/ppermute | solution.py:182
  424.2 233.5 %collective-permute-start.17 = (bf16[1024,1024]{1,0:T(8,128)(2,1)}, bf16[1024,1024]{1,0:T(8,128)(2,1)}, u32[]{:S(2)}, u32[]{:S(2)}) collective-permute-start(bf16[1024,1024]{1,0:T(8,128)(2,1)} %collective-permute-done.3.refs_1_), channel_id=1, source_target_pairs={{0,8},{8,16},{16,24},{24,0},{1,9},{9,17},{17,25},{25,1},{2,10},{10... | collective-permute-start | bytes 6291464 | tf_op jit(solution)/shard_map/ppermute | solution.py:174
  431.7 229.8 %collective-permute-start.18 = (bf16[1024,1024]{1,0:T(8,128)(2,1)}, bf16[1024,1024]{1,0:T(8,128)(2,1)}, u32[]{:S(2)}, u32[]{:S(2)}) collective-permute-start(bf16[1024,1024]{1,0:T(8,128)(2,1)} %collective-permute-done.14.refs_1_), channel_id=1, source_target_pairs={{0,8},{8,16},{16,24},{24,0},{1,9},{9,17},{17,25},{25,1},{2,10},{10... | collective-permute-start | bytes 6291464 | tf_op jit(solution)/shard_map/ppermute | solution.py:174
  432.5 232.8 %collective-permute-start.10 = (bf16[512,2048]{1,0:T(8,128)(2,1)S(1)}, bf16[512,2048]{1,0:T(8,128)(2,1)}, u32[]{:S(2)}, u32[]{:S(2)}) collective-permute-start(bf16[512,2048]{1,0:T(8,128)(2,1)S(1)} %copy-done.1), channel_id=1, source_target_pairs={{0,8},{8,16},{16,24},{24,0},{1,9},{9,17},{17,25},{25,1},{2,10},{10... | collective-permute-start | bytes 6291464 | tf_op jit(solution)/shard_map/ppermute | solution.py:174
  433.1 234.8 %collective-permute-start.11 = (bf16[512,2048]{1,0:T(8,128)(2,1)}, bf16[512,2048]{1,0:T(8,128)(2,1)}, u32[]{:S(2)}, u32[]{:S(2)}) collective-permute-start(bf16[512,2048]{1,0:T(8,128)(2,1)} %collective-permute-done.4.refs_1_), channel_id=1, source_target_pairs={{0,8},{8,16},{16,24},{24,0},{1,9},{9,17},{17,25},{25,1},{2,10},{10... | collective-permute-start | bytes 6291464 | tf_op jit(solution)/shard_map/ppermute | solution.py:174
  433.2 187.0 %collective-permute-start.12 = (bf16[128,2048]{1,0:T(8,128)(2,1)}, bf16[128,2048]{1,0:T(8,128)(2,1)S(1)}, u32[]{:S(2)}, u32[]{:S(2)}) collective-permute-start(bf16[128,2048]{1,0:T(8,128)(2,1)} %collective-permute-done.6.refs_1_), channel_id=1, source_target_pairs={{0,8},{8,16},{16,24},{24,0},{1,9},{9,17},{17,25},{25,1},{2,10},{10... | collective-permute-start | bytes 1572872 | tf_op jit(solution)/shard_map/ppermute | solution.py:174
  620.2 7.0 %collective-permute-start.21 = (bf16[2048]{0:T(1024)(128)(2,1)S(1)}, bf16[2048]{0:T(1024)(128)(2,1)S(1)}, u32[]{:S(2)}, u32[]{:S(2)}) collective-permute-start(bf16[2048]{0:T(1024)(128)(2,1)S(1)} %collective-permute-done.20), channel_id=1, source_target_pairs={{0,8},{8,16},{16,24},{24,0},{1,9},{9,17},{17,25},{25,1},{2,10},{10... | collective-permute-start | bytes 12296 | tf_op jit(solution)/shard_map/ppermute | solution.py:182
  627.2 14.3 %collective-permute-start.16 = (bf16[128,2048]{1,0:T(8,128)(2,1)S(1)}, bf16[128,2048]{1,0:T(8,128)(2,1)S(1)}, u32[]{:S(2)}, u32[]{:S(2)}) collective-permute-start(bf16[128,2048]{1,0:T(8,128)(2,1)S(1)} %collective-permute-done.12.refs_1_), channel_id=1, source_target_pairs={{0,8},{8,16},{16,24},{24,0},{1,9},{9,17},{17,25},{25,1},{2,10},{10... | collective-permute-start | bytes 1572872 | tf_op jit(solution)/shard_map/ppermute | solution.py:174
  641.4 13.6 %collective-permute-start.15 = (bf16[128,2048]{1,0:T(8,128)(2,1)}, bf16[128,2048]{1,0:T(8,128)(2,1)S(1)}, u32[]{:S(2)}, u32[]{:S(2)}) collective-permute-start(bf16[128,2048]{1,0:T(8,128)(2,1)} %copy-done.4), channel_id=1, source_target_pairs={{0,8},{8,16},{16,24},{24,0},{1,9},{9,17},{17,25},{25,1},{2,10},{10... | collective-permute-start | bytes 1572872 | tf_op jit(solution)/shard_map/ppermute | solution.py:174
  (10 other events, 396.6 us)
